TPU v7x, 256 devices: a whole 4x4x8 slice. The times are simulated.
256 devices in a mesh: dp: 32 (over z, x), parity: 8 (over y, core).
Axes of the slice: x: 4, y: 4, z: 8, core: 2. Of those that a mesh axis runs over, the one named last changes fastest.
Arguments:
- first_moment: float32 [131072, 512], P(('dp', 'parity')), may hold values from -6 to 6
- second_moment: float32 [131072, 512], P(('dp', 'parity')), may hold values from 0.01 to 4
- new_owner: int32 [131072, 1], P(('dp', 'parity')), may hold values from 0 to 31; in each aligned block of 512 rows (0 to 511, 512 to 1023, ...) at most 20 rows name the same one
- code_index: int32 [2, 8], replicated, may hold values from 0 to 7
Outputs:
- new_first: float32 [163840, 512], P(('dp', 'parity'))
- new_second: float32 [163840, 512], P(('dp', 'parity'))
- parity: float32 [20480, 2048], P(('dp', 'parity'))
- loads: int32 [32, 8], P('dp', 'parity')
Inputs may be any that keep to these rules, and one draw needn't show every extreme that they name: `new_owner`: in the rows of one device (aligned blocks of 512 rows) no owner is named more than 20 times, a bound that some owner reaches in some blocks.
All inputs are finite; a program needn't handle non-finite values.
Results may differ from a plain program's by a relative error of at most 0.0003.
Values sent between devices are 32-bit elements; how exact they have to be, the bound alone decides.
A program may use at most 64 MiB of HBM per device.

v0:
```python
import jax
import jax.numpy as jnp
from jax import lax
from jax.sharding import Mesh
from jax.sharding import PartitionSpec as P

DP = ("dp_0", "dp_1")
DP_PARITY = ("dp_0", "dp_1", "parity")


def one_axis_at_a_time(array, axes):
    for axis in axes:
        array = lax.psum(array, axis)
    return array


def in_one_piece(arrays, axis, split_dim, concat_dim, along):
    widths = [a.shape[along] for a in arrays]
    both = jnp.concatenate(arrays, axis=along)
    result = lax.all_to_all(both, axis, split_axis=split_dim, concat_axis=concat_dim, tiled=True)
    return tuple(jnp.split(result, [sum(widths[:k]) for k in range(1, len(widths))], axis=along))


def body(first_moment, second_moment, new_owner, code_index):
    held = first_moment.shape[0]
    width = first_moment.shape[1]
    owners_count = lax.axis_size(DP)
    members = lax.axis_size("parity")
    room = held // owners_count + max(1, held // (4 * owners_count))
    capacity = owners_count * room
    owner = new_owner[:, 0]
    onehot = (owner[:, None] == jnp.arange(owners_count, dtype=jnp.int32)[None, :]).astype(
        jnp.int32
    )
    before = jnp.cumsum(onehot, axis=0) - onehot
    rank = jnp.sum(before * onehot, axis=1)
    target = owner * room + rank
    send_first = jnp.zeros((capacity, width), jnp.float32).at[target].set(first_moment)
    send_second = jnp.zeros((capacity, width), jnp.float32).at[target].set(second_moment)
    counts = jnp.sum(onehot, axis=0)
    got_first, got_second = (
        lax.all_to_all(send_first, DP, split_axis=0, concat_axis=0, tiled=True),
        lax.all_to_all(send_second, DP, split_axis=0, concat_axis=0, tiled=True),
    )
    totals = one_axis_at_a_time(counts, DP)
    mine = lax.dynamic_slice_in_dim(totals, lax.axis_index(DP), 1, 0)
    loads = jnp.reshape(mine, (1, 1))
    coef = code_index.astype(jnp.float32) * 0.25
    units = coef.shape[0]
    rows = capacity // members
    share_first, share_second = in_one_piece((got_first, got_second), "parity", 0, 0, 1)
    joined = jnp.concatenate(
        [share_first.reshape(members, rows, width), share_second.reshape(members, rows, width)],
        axis=2,
    )
    parity = jnp.einsum("rp,psc->src", coef, joined, precision=lax.Precision.HIGHEST)
    parity = parity.reshape(rows, units * 2 * width)
    return (got_first, got_second, parity, loads)


def solution(mesh):
    finer = Mesh(mesh.devices.reshape(8, 4, mesh.shape["parity"]), ("dp_0", "dp_1", "parity"))
    in_specs = (P(DP_PARITY, None), P(DP_PARITY, None), P(DP_PARITY, None), P())
    out_specs = (P(DP_PARITY, None), P(DP_PARITY, None), P(DP_PARITY, None), P(DP, "parity"))
    return jax.shard_map(body, mesh=finer, in_specs=in_specs, out_specs=out_specs, check_vma=False)
```

profile of v0, /device:TPU:13, one launch (start us, length us, event | category | flops | bytes accessed | tf_op | source)
XLA Modules:
  0.0 150.6 jit_solution(16433175476554826125)
XLA Ops:
  0.6 0.7 fusion.10
  1.3 1.2 reduce-window.6
  2.5 0.2 slice_reduce_fusion
  2.7 0.9 convert_reduce_fusion
  3.6 0.7 compare_select_fusion
  4.3 3.2 %scatter_custom_fusion = f32[640,512]{1,0:T(8,128)S(1)} fusion(s32[512]{0:T(512)S(1)} %bitcast.34, f32[512,512]{1,0:T(8,128)} %param.4, f32[]{:T(128)} %constant.10.clone.1), kind=kCustom, calls=%fused_computation.9 | custom fusion | bytes 1311232 | tf_op jit(solution)/shard_map/scatter | solution.py:38
  7.6 1.3 all_to_all.22
  8.9 11.0 %all-to-all-start = ((f32[32,20,512]{2,1,0:T(8,128)}), f32[32,20,512]{2,1,0:T(8,128)S(1)}, u32[]{:S(2)}, u32[]{:S(2)}) async-start(f32[32,20,512]{2,1,0:T(8,128)} %all_to_all.22), calls=%async_computation | async-start | bytes 3145728 | tf_op jit(solution)/shard_map/all_to_all | solution.py:42
  19.9 3.2 %scatter_custom_fusion.1 = f32[640,512]{1,0:T(8,128)S(1)} fusion(s32[512]{0:T(512)S(1)} %bitcast.35, f32[512,512]{1,0:T(8,128)} %param.5, f32[]{:T(128)} %constant.10.clone.1), kind=kCustom, calls=%fused_computation.7 | custom fusion | bytes 1311232 | tf_op jit(solution)/shard_map/scatter | solution.py:39
  23.1 1.3 all_to_all.25
  24.4 34.4 %all-to-all-done = f32[32,20,512]{2,1,0:T(8,128)S(1)} async-done(((f32[32,20,512]{2,1,0:T(8,128)}), f32[32,20,512]{2,1,0:T(8,128)S(1)}, u32[]{:S(2)}, u32[]{:S(2)}) %all-to-all-start) | async-done | bytes 1310752 | tf_op jit(solution)/shard_map/all_to_all | solution.py:42
  58.9 4.8 %all-to-all-start.1 = ((f32[32,20,512]{2,1,0:T(8,128)}), f32[32,20,512]{2,1,0:T(8,128)S(1)}, u32[]{:S(2)}, u32[]{:S(2)}) async-start(f32[32,20,512]{2,1,0:T(8,128)} %all_to_all.25), calls=%async_computation.1 | async-start | bytes 3145728 | tf_op jit(solution)/shard_map/all_to_all | solution.py:43
  63.6 1.2 concatenate.11
  64.8 36.9 %all-to-all-done.1 = f32[32,20,512]{2,1,0:T(8,128)S(1)} async-done(((f32[32,20,512]{2,1,0:T(8,128)}), f32[32,20,512]{2,1,0:T(8,128)S(1)}, u32[]{:S(2)}, u32[]{:S(2)}) %all-to-all-start.1) | async-done | bytes 1310752 | tf_op jit(solution)/shard_map/all_to_all | solution.py:43
  101.7 1.2 concatenate.12
  102.9 3.5 %pad_maximum_fusion = f32[8,80,1024]{2,1,0:T(8,128)} fusion(f32[8,80,512]{2,1,0:T(8,128)} %concatenate.12, f32[8,80,512]{2,1,0:T(8,128)} %concatenate.11), kind=kLoop, calls=%fused_computation.2 | loop fusion | flops 655360 | bytes 5242880 | tf_op jit(solution)/shard_map/concatenate | solution.py:19
  106.4 6.5 %all-to-all-start.2 = ((f32[8,80,1024]{2,1,0:T(8,128)}), f32[8,80,1024]{2,1,0:T(8,128)}, u32[]{:S(2)}, u32[]{:S(2)}) async-start(f32[8,80,1024]{2,1,0:T(8,128)} %pad_maximum_fusion), calls=%async_computation.2 | async-start | bytes 5242880 | tf_op jit(solution)/shard_map/all_to_all | solution.py:20
  112.9 8.8 %psum.14 = s32[32]{0:T(128)S(1)} all-reduce(s32[32]{0:T(128)S(1)} %get-tuple-element.4), channel_id=1, replica_groups=mesh['dp_0'=8,'dp_1'=4,'parity'=8] {'dp_0'}, use_global_device_ids=true, to_apply=%region_6.7 | all-reduce | flops 32 | bytes 256 | tf_op jit(solution)/shard_map/psum | solution.py:13
  121.7 4.8 %psum.15 = s32[32]{0:T(128)S(1)} all-reduce(s32[32]{0:T(128)S(1)} %psum.14), channel_id=1, replica_groups=mesh['dp_0'=8,'dp_1'=4,'parity'=8] {'dp_1'}, use_global_device_ids=true, to_apply=%region_7.8 | all-reduce | flops 32 | bytes 256 | tf_op jit(solution)/shard_map/psum | solution.py:13
  126.5 0.6 dynamic_slice.3
  127.1 1.2 all_to_all.24
  128.3 1.2 all_to_all.27
  129.4 14.3 %all-to-all-done.2 = f32[8,80,1024]{2,1,0:T(8,128)} async-done(((f32[8,80,1024]{2,1,0:T(8,128)}), f32[8,80,1024]{2,1,0:T(8,128)}, u32[]{:S(2)}, u32[]{:S(2)}) %all-to-all-start.2) | async-done | bytes 2621472 | tf_op jit(solution)/shard_map/all_to_all | solution.py:20
  143.7 1.9 %fusion.17 = (f32[640,512]{1,0:T(8,128)S(1)}, f32[640,512]{1,0:T(8,128)S(1)}) fusion(f32[640,1024]{1,0:T(8,128)} %bitcast.5), kind=kLoop, calls=%fused_computation.28 | loop fusion | bytes 5242880 | tf_op jit(solution)/shard_map/split | solution.py:21
  145.7 0.8 copy.9
  146.5 0.0 copy-start
  146.5 0.8 copy.10
  147.3 0.0 copy-done
  147.3 2.3 %fusion = f32[80,1024,2]{1,2,0:T(2,128)S(1)} fusion(f32[8,80,512]{2,0,1:T(8,128)S(1)} %copy.10, f32[8,80,512]{2,0,1:T(8,128)S(1)} %copy.9, s32[2,8]{1,0:T(2,128)S(1)} %copy-done), kind=kOutput, calls=%fused_computation.3 | convolution fusion | flops 16384032 | bytes 3276864 | tf_op jit(solution)/shard_map/rp,psc->src/dot_general | solution.py:56
  149.6 1.0 copy.12
  (2 shorter events, 0.0 us)
Async XLA Ops:
  8.9 50.0 %all-to-all-start = ((f32[32,20,512]{2,1,0:T(8,128)}), f32[32,20,512]{2,1,0:T(8,128)S(1)}, u32[]{:S(2)}, u32[]{:S(2)}) async-start(f32[32,20,512]{2,1,0:T(8,128)} %all_to_all.22), calls=%async_computation | async-start | bytes 3145728 | tf_op jit(solution)/shard_map/all_to_all | solution.py:42
  58.9 42.8 %all-to-all-start.1 = ((f32[32,20,512]{2,1,0:T(8,128)}), f32[32,20,512]{2,1,0:T(8,128)S(1)}, u32[]{:S(2)}, u32[]{:S(2)}) async-start(f32[32,20,512]{2,1,0:T(8,128)} %all_to_all.25), calls=%async_computation.1 | async-start | bytes 3145728 | tf_op jit(solution)/shard_map/all_to_all | solution.py:43
  106.4 37.3 %all-to-all-start.2 = ((f32[8,80,1024]{2,1,0:T(8,128)}), f32[8,80,1024]{2,1,0:T(8,128)}, u32[]{:S(2)}, u32[]{:S(2)}) async-start(f32[8,80,1024]{2,1,0:T(8,128)} %pad_maximum_fusion), calls=%async_computation.2 | async-start | bytes 5242880 | tf_op jit(solution)/shard_map/all_to_all | solution.py:20
  146.5 0.8 copy-start
where the time goes:
time: 153 us; the launch traced here: 151 us
  waiting for transfers between devices  85.6 us (56%)
  starting transfers between devices  22.3 us (15%)
  local copies, waits for them, and re-layouts  19.1 us (12%)
  blocking collectives  13.6 us (9%)
  other arithmetic  7 us (5%)
  matrix products  2.29 us (1%)
    all_to_all x1, waiting for transfers between devices, body(): lax.all_to_all(send_second, DP, split_axis=0, concat_axis=0, tiled=True)  36.9 us
    all_to_all x1, waiting for transfers between devices, body(): lax.all_to_all(send_first, DP, split_axis=0, concat_axis=0, tiled=True)  34.4 us
    all_to_all x1, waiting for transfers between devices, in_one_piece(): lax.all_to_all(both, axis, split_axis=split_dim, concat_axis=concat_dim,...  14.3 us
    psum x2, blocking collectives, one_axis_at_a_time(): array = lax.psum(array, axis)  13.6 us
    all_to_all x1, starting transfers between devices, body(): lax.all_to_all(send_first, DP, split_axis=0, concat_axis=0, tiled=True)  11 us
    all_to_all x1, starting transfers between devices, in_one_piece(): lax.all_to_all(both, axis, split_axis=split_dim, concat_axis=concat_dim,...  6.47 us
    all_to_all x1, starting transfers between devices, body(): lax.all_to_all(send_second, DP, split_axis=0, concat_axis=0, tiled=True)  4.76 us
    concatenate x1, other arithmetic, in_one_piece(): both = jnp.concatenate(arrays, axis=along)  3.53 us
  transfers between devices with their start and end apart: 3, of which 3 were waited for; matrix products, arithmetic and copies ran while one was open for 3% of the time, Pallas kernels for 0%

commit v1 on v0

v1 whole, which is shorter than its diff:
```python
import functools

import jax
import jax.numpy as jnp
from jax import lax
from jax.experimental import pallas as pl
from jax.experimental.pallas import tpu as pltpu
from jax.sharding import PartitionSpec as P

MESH = pl.DeviceIdType.MESH
NZ, NX = 8, 4
N_DP = NZ * NX
N_PAR = 8
ROOM = 20
BLK = 512
WIDTH = 512
PAIR = 2 * ROOM
GROUP = 8
LANE = 32


def exchange(first_hbm, second_hbm, owner_ref, code_ref,
             new_first, new_second, parity, loads,
             x_first, x_second, parts, send, recv, share, cnt_send, cnt_recv,
             in_sem, send_sem, recv_sem, cs_sem, cr_sem, ps_sem, pr_sem):
    me = lax.axis_index("dp")
    col = lax.axis_index("parity")
    z = lax.div(me, NX)
    x = lax.rem(me, NX)

    loads_in = [
        pltpu.make_async_copy(first_hbm, x_first, in_sem.at[0]),
        pltpu.make_async_copy(second_hbm, x_second, in_sem.at[1]),
    ]
    for c in loads_in:
        c.start()

    barrier = pltpu.get_barrier_semaphore()
    for k in range(1, N_DP):
        pl.semaphore_signal(barrier, inc=1, device_id={"dp": lax.rem(me + k, N_DP)}, device_id_type=MESH)
    for k in range(1, N_PAR):
        pl.semaphore_signal(barrier, inc=1, device_id={"parity": lax.rem(col + k, N_PAR)}, device_id_type=MESH)

    owner = owner_ref[...]
    onehot = (lax.broadcasted_iota(jnp.int32, (N_DP, BLK), 0) == owner).astype(jnp.float32)
    earlier = lax.broadcasted_iota(jnp.int32, (BLK, BLK), 0) < lax.broadcasted_iota(jnp.int32, (BLK, BLK), 1)
    before = jnp.dot(onehot.astype(jnp.bfloat16), earlier.astype(jnp.float32).astype(jnp.bfloat16),
                     preferred_element_type=jnp.float32)
    rank = jnp.sum(before * onehot, axis=0, keepdims=True)
    key = owner.astype(jnp.float32) * LANE + rank
    counts = jnp.sum(onehot, axis=1, keepdims=True).astype(jnp.int32)
    counts = jnp.broadcast_to(counts, (N_DP, 128))
    for d in range(N_DP):
        cnt_send[d] = counts[d:d + 1]

    for m, (c, src) in enumerate(zip(loads_in, (x_first, x_second))):
        c.wait()
        whole = src[...]
        high = whole.astype(jnp.bfloat16)
        rest = whole - high.astype(jnp.float32)
        mid = rest.astype(jnp.bfloat16)
        parts[3 * m] = high
        parts[3 * m + 1] = mid
        parts[3 * m + 2] = (rest - mid.astype(jnp.float32)).astype(jnp.bfloat16)

    rows = 24
    shape = (GROUP, rows, BLK)
    slot = (lax.broadcasted_iota(jnp.int32, shape, 0) * LANE + lax.broadcasted_iota(jnp.int32, shape, 1))
    slot = slot.reshape(GROUP * rows, BLK).astype(jnp.float32)

    def build(g, carry):
        base = key - (g * (GROUP * LANE)).astype(jnp.float32)
        chosen = []
        for m in range(2):
            pick = jnp.where(slot == base + 4.0 * m, 1.0, 0.0).astype(jnp.bfloat16)
            out = jnp.dot(pick, parts[3 * m], preferred_element_type=jnp.float32)
            out = out + jnp.dot(pick, parts[3 * m + 1], preferred_element_type=jnp.float32)
            out = out + jnp.dot(pick, parts[3 * m + 2], preferred_element_type=jnp.float32)
            chosen.append(out.reshape(GROUP, rows, WIDTH))
        a, b = chosen
        for o in range(GROUP):
            d = g * GROUP + o
            send[d, 0:16] = a[o, 0:16]
            send[d, 16:24] = a[o, 16:24] + b[o, 0:8]
            send[d, 24:40] = b[o, 8:24]
        return carry

    lax.fori_loop(0, N_DP // GROUP, build, 0)
    pl.semaphore_wait(barrier, N_DP - 1 + N_PAR - 1)

    def step(i):
        i = lax.rem(i + col, NZ)
        half = lax.div(i, 2)
        return jnp.where(lax.rem(i, 2) == 0, half, NZ - 1 - half)

    def ids(i, dx):
        dz = step(i)
        to = lax.rem(z + dz, NZ) * NX + lax.rem(x + dx, NX)
        source_z = lax.rem(z - dz + NZ, NZ)
        source_x = lax.rem(x - dx + NX, NX)
        return dz, dz * NX + dx, to, source_z, source_x

    def block_copy(to, k, landing):
        return pltpu.make_async_remote_copy(
            src_ref=send.at[to], dst_ref=recv.at[landing], send_sem=send_sem.at[k], recv_sem=recv_sem.at[k],
            device_id={"dp": to}, device_id_type=MESH)

    def count_copy(to, k, landing):
        return pltpu.make_async_remote_copy(
            src_ref=cnt_send.at[to], dst_ref=cnt_recv.at[landing], send_sem=cs_sem.at[k], recv_sem=cr_sem.at[k],
            device_id={"dp": to}, device_id_type=MESH)

    def share_copy(source, source_x, target, from_col):
        return pltpu.make_async_remote_copy(
            src_ref=recv.at[source], dst_ref=share.at[from_col * NX + source_x],
            send_sem=ps_sem.at[source], recv_sem=pr_sem.at[from_col * NX + source_x],
            device_id={"parity": target}, device_id_type=MESH)

    def issue(i, carry):
        for dx in range(NX):
            dz, k, to, _, _ = ids(i, dx)

            @pl.when(k != 0)
            def _():
                block_copy(to, k, me).start()
                count_copy(to, k, me).start()
        return carry

    lax.fori_loop(0, NZ, issue, 0)
    recv[me] = send[me]
    cnt_recv[me] = cnt_send[me]

    def arrive(i, carry):
        for dx in range(NX):
            dz, k, to, sz, sx = ids(i, dx)
            source = sz * NX + sx

            @pl.when(k != 0)
            def _():
                block_copy(to, k, source).wait_recv()

            @pl.when(sz != col)
            def _():
                share_copy(source, sx, sz, col).start()

            @pl.when(sz == col)
            def _():
                share[col * NX + sx] = recv[source]
        for h in range(NX // 2):
            one, two = sz * NX + 2 * h, sz * NX + 2 * h + 1
            at = pl.ds(pl.multiple_of((sz * (NX // 2) + h) * PAIR, 8), PAIR)
            new_first[at] = jnp.concatenate([recv[one, 0:ROOM], recv[two, 0:ROOM]], axis=0)
            new_second[at] = jnp.concatenate([recv[one, ROOM:PAIR], recv[two, ROOM:PAIR]], axis=0)
        return carry

    lax.fori_loop(0, NZ, arrive, 0)

    def counted(i, carry):
        for dx in range(NX):
            _, k, to, sz, sx = ids(i, dx)

            @pl.when(k != 0)
            def _():
                count_copy(to, k, sz * NX + sx).wait()
                block_copy(to, k, sz * NX + sx).wait_send()
        return carry

    lax.fori_loop(0, NZ, counted, 0)
    total = cnt_recv[0]
    for d in range(1, N_DP):
        total = total + cnt_recv[d]
    loads[...] = total

    def shared(other, carry):
        @pl.when(other != col)
        def _():
            for sx in range(NX):
                share_copy(other * NX + sx, sx, other, other).wait_recv()
                share_copy(other * NX + sx, sx, other, col).wait_send()
        return carry

    lax.fori_loop(0, N_PAR, shared, 0)
    coef = [[code_ref[r, p].astype(jnp.float32) * 0.25 for p in range(N_PAR)] for r in range(2)]
    for h in range(NX // 2):
        sums = [[None, None], [None, None]]
        for r in range(2):
            for o in range(2):
                acc = coef[r][0] * share[2 * h + o]
                for p in range(1, N_PAR):
                    acc = acc + coef[r][p] * share[p * NX + 2 * h + o]
                sums[r][o] = acc
        for r in range(2):
            one, two = sums[r]
            at = slice(h * PAIR, (h + 1) * PAIR)
            parity[at, (2 * r) * WIDTH:(2 * r + 1) * WIDTH] = jnp.concatenate([one[0:ROOM], two[0:ROOM]], axis=0)
            parity[at, (2 * r + 1) * WIDTH:(2 * r + 2) * WIDTH] = jnp.concatenate([one[ROOM:PAIR], two[ROOM:PAIR]], axis=0)


def put_out(nf, ns, par, cnt, nf_out, ns_out, par_out, cnt_out, sem):
    copies = [
        pltpu.make_async_copy(nf, nf_out, sem.at[0]),
        pltpu.make_async_copy(ns, ns_out, sem.at[1]),
        pltpu.make_async_copy(par, par_out, sem.at[2]),
    ]
    for c in copies:
        c.start()
    cnt_out[...] = cnt[0:1, 0:1]
    for c in copies:
        c.wait()


def body(first_moment, second_moment, new_owner, code_index):
    f32, i32 = jnp.float32, jnp.int32
    capacity = N_DP * ROOM
    vmem = pl.BlockSpec(memory_space=pltpu.VMEM)
    anywhere = pl.BlockSpec(memory_space=pl.ANY)
    dma = pltpu.SemaphoreType.DMA
    held = pl.pallas_call(
        exchange,
        out_shape=(jax.ShapeDtypeStruct((capacity, WIDTH), f32), jax.ShapeDtypeStruct((capacity, WIDTH), f32),
                   jax.ShapeDtypeStruct((capacity // N_PAR, 4 * WIDTH), f32), jax.ShapeDtypeStruct((1, 128), i32)),
        in_specs=[anywhere, anywhere, vmem, pl.BlockSpec(memory_space=pltpu.SMEM)],
        out_specs=(vmem, vmem, vmem, vmem),
        scratch_shapes=[
            pltpu.VMEM((BLK, WIDTH), f32), pltpu.VMEM((BLK, WIDTH), f32), pltpu.VMEM((6, BLK, WIDTH), jnp.bfloat16),
            pltpu.VMEM((N_DP, PAIR, WIDTH), f32), pltpu.VMEM((N_DP, PAIR, WIDTH), f32),
            pltpu.VMEM((N_PAR * NX, PAIR, WIDTH), f32),
            pltpu.VMEM((N_DP, 1, 128), i32), pltpu.VMEM((N_DP, 1, 128), i32),
            dma((2,)), dma((N_DP,)), dma((N_DP,)), dma((N_DP,)), dma((N_DP,)), dma((N_DP,)), dma((N_DP,)),
        ],
        compiler_params=pltpu.CompilerParams(collective_id=0, has_side_effects=True, vmem_limit_bytes=32 * 2**20),
    )(first_moment, second_moment, new_owner.reshape(1, BLK), code_index)
    return pl.pallas_call(
        put_out,
        out_shape=(jax.ShapeDtypeStruct((capacity, WIDTH), f32), jax.ShapeDtypeStruct((capacity, WIDTH), f32),
                   jax.ShapeDtypeStruct((capacity // N_PAR, 4 * WIDTH), f32), jax.ShapeDtypeStruct((1, 1), i32)),
        in_specs=[vmem, vmem, vmem, vmem],
        out_specs=(anywhere, anywhere, anywhere, vmem),
        scratch_shapes=[dma((3,))],
        compiler_params=pltpu.CompilerParams(vmem_limit_bytes=16 * 2**20),
    )(*held)


def solution(mesh):
    rows = P(("dp", "parity"), None)
    return jax.shard_map(body, mesh=mesh, in_specs=(rows, rows, rows, P()),
                         out_specs=(rows, rows, rows, P("dp", "parity")), check_vma=False)
```

time: 153 us -> 92.8 us (0.61)
  the two profiles are of different devices: /device:TPU:13 before, /device:TPU:1 now
where the time goes in v1:
time: 92.8 us; the launch traced here: 92.6 us
  Pallas kernels  88.2 us (95%)
  local copies, waits for them, and re-layouts  3.8 us (4%)
    pallas_call x1, Pallas kernels, body(): pl.pallas_call(exchange, out_shape=(jax.ShapeDtypeStruct((capacity, WIDTH...  85.9 us
    unnamed x8, local copies, waits for them, and re-layouts  3.8 us
    pallas_call x1, Pallas kernels, body(): pl.pallas_call(put_out, out_shape=(jax.ShapeDtypeStruct((capacity, WIDTH)...  2.24 us

profile of v1, /device:TPU:1, one launch (start us, length us, event | category | flops | bytes accessed | tf_op | source)
XLA Modules:
  0.0 92.6 jit_solution(14920538752917168859)
XLA Ops:
  0.6 0.0 copy-start
  0.6 1.2 %copy-done = f32[512,512]{1,0:T(8,128)S(1)} copy-done((f32[512,512]{1,0:T(8,128)S(1)}, f32[512,512]{1,0:T(8,128)}, u32[]{:S(2)}) %copy-start) | copy-done | bytes 1048600
  1.9 0.0 copy-start.1
  1.9 1.2 %copy-done.1 = f32[512,512]{1,0:T(8,128)S(1)} copy-done((f32[512,512]{1,0:T(8,128)S(1)}, f32[512,512]{1,0:T(8,128)}, u32[]{:S(2)}) %copy-start.1) | copy-done | bytes 1048600
  3.1 0.0 copy-start.2
  3.1 0.7 copy-done.2
  3.8 0.0 copy-start.3
  3.8 0.7 copy-done.3
  4.4 85.9 %shard_map.75 = (f32[640,512]{1,0:T(8,128)S(1)}, f32[640,512]{1,0:T(8,128)S(1)}, f32[80,2048]{1,0:T(8,128)S(1)}, s32[1,128]{1,0:T(1,128)S(1)}) custom-call(f32[512,512]{1,0:T(8,128)S(1)} %copy-done, f32[512,512]{1,0:T(8,128)S(1)} %copy-done.1, s32[1,512]{1,0:T(1,128)S(1)} %bitcast.1, s32[2,8]{1,0:T(2,128)S(1)} %copy-done.3), custom_call_target="tpu_custom_call" | custom-call | tf_op jit(solution)/shard_map/pallas_call | solution.py:218
  90.4 2.2 %shard_map.76 = (f32[640,512]{1,0:T(8,128)}, f32[640,512]{1,0:T(8,128)}, f32[80,2048]{1,0:T(8,128)}, s32[1,1]{1,0:T(1,128)}) custom-call(f32[640,512]{1,0:T(8,128)S(1)} %get-tuple-element.8.nf, f32[640,512]{1,0:T(8,128)S(1)} %get-tuple-element.9.ns, f32[80,2048]{1,0:T(8,128)S(1)} %get-tuple-element.10.par, s32[1,128]{1,0:T(1,128)S(1)} %get-tuple-element.11.cnt), custom_call_target="tpu_custom_call" | custom-call | tf_op jit(solution)/shard_map/pallas_call | solution.py:233
Async XLA Ops:
  0.6 1.2 %copy-start = (f32[512,512]{1,0:T(8,128)S(1)}, f32[512,512]{1,0:T(8,128)}, u32[]{:S(2)}) copy-start(f32[512,512]{1,0:T(8,128)} %first_hbm.1) | copy-start | bytes 3145732
  1.9 1.2 %copy-start.1 = (f32[512,512]{1,0:T(8,128)S(1)}, f32[512,512]{1,0:T(8,128)}, u32[]{:S(2)}) copy-start(f32[512,512]{1,0:T(8,128)} %second_hbm.1) | copy-start | bytes 3145732
  3.1 0.7 copy-start.2
  3.8 0.7 copy-start.3

commit v2 on v1

v2 whole, which is shorter than its diff:
```python
import functools

import jax
import jax.numpy as jnp
from jax import lax
from jax.experimental import pallas as pl
from jax.experimental.pallas import tpu as pltpu
from jax.sharding import PartitionSpec as P

MESH = pl.DeviceIdType.MESH
NZ, NX = 8, 4
N_DP = NZ * NX
N_PAR = 8
ROOM = 20
BLK = 512
WIDTH = 512
PAIR = 2 * ROOM
GROUP = 8
PIECES = 4
LANE = 32


def by_class(classes):
    steps = [(0, dx) for dx in range(1, NX)]
    for c in classes:
        for dx in range(NX):
            steps += [(c, dx)] if 2 * c == NZ else [(c, dx), (NZ - c, dx)]
    return [dz * NX + dx for dz, dx in steps]


ISSUE = (by_class((1, 2, 3, 4)), by_class((3, 4, 1, 2)))
WAIT = ISSUE
DONE = tuple([max(w.index(k) for k in range(dz * NX, dz * NX + NX) if k) for dz in range(NZ)] for w in WAIT)
PLANES = tuple(sorted(range(NZ), key=done.__getitem__) for done in DONE)
PLACED = [max(done[planes[j]] for done, planes in zip(DONE, PLANES)) for j in range(NZ)]


def exchange(first_hbm, second_hbm, owner_hbm, code_hbm,
             new_first, new_second, parity, loads,
             owner_ref, code_ref, x_first, x_second, parts, send, recv, share, sums, cnt_send, cnt_recv,
             in_sem, send_sem, recv_sem, cs_sem, cr_sem, ps_sem, pr_sem):
    me = lax.axis_index("dp")
    col = lax.axis_index("parity")
    z = lax.div(me, NX)
    x = lax.rem(me, NX)

    loads_in = [
        pltpu.make_async_copy(first_hbm, x_first, in_sem.at[0]),
        pltpu.make_async_copy(second_hbm, x_second, in_sem.at[1]),
    ]
    small_in = [
        pltpu.make_async_copy(owner_hbm, owner_ref, in_sem.at[2]),
        pltpu.make_async_copy(code_hbm, code_ref, in_sem.at[3]),
    ]
    for c in small_in + loads_in:
        c.start()

    barrier = pltpu.get_barrier_semaphore()
    for k in range(1, N_DP):
        pl.semaphore_signal(barrier, inc=1, device_id={"dp": lax.rem(me + k, N_DP)}, device_id_type=MESH)
    for k in range(1, N_PAR):
        pl.semaphore_signal(barrier, inc=1, device_id={"parity": lax.rem(col + k, N_PAR)}, device_id_type=MESH)

    for c in small_in:
        c.wait()
    owner = owner_ref[...]
    onehot = (lax.broadcasted_iota(jnp.int32, (N_DP, BLK), 0) == owner).astype(jnp.float32)
    earlier = lax.broadcasted_iota(jnp.int32, (BLK, BLK), 0) < lax.broadcasted_iota(jnp.int32, (BLK, BLK), 1)
    before = jnp.dot(onehot.astype(jnp.bfloat16), earlier.astype(jnp.float32).astype(jnp.bfloat16),
                     preferred_element_type=jnp.float32)
    rank = jnp.sum(before * onehot, axis=0, keepdims=True)
    key = owner.astype(jnp.float32) * LANE + rank
    counts = jnp.sum(onehot, axis=1, keepdims=True).astype(jnp.int32)
    counts = jnp.broadcast_to(counts, (N_DP, 128))
    for d in range(N_DP):
        cnt_send[d] = counts[d:d + 1]

    for m, (c, src) in enumerate(zip(loads_in, (x_first, x_second))):
        c.wait()
        whole = src[...]
        high = whole.astype(jnp.bfloat16)
        rest = whole - high.astype(jnp.float32)
        mid = rest.astype(jnp.bfloat16)
        parts[3 * m] = high
        parts[3 * m + 1] = mid
        parts[3 * m + 2] = (rest - mid.astype(jnp.float32)).astype(jnp.bfloat16)

    rows = 24
    shape = (GROUP, rows, BLK)
    slot = (lax.broadcasted_iota(jnp.int32, shape, 0) * LANE + lax.broadcasted_iota(jnp.int32, shape, 1))
    slot = slot.reshape(GROUP * rows, BLK).astype(jnp.float32)

    def build(g, carry):
        base = key - (g * (GROUP * LANE)).astype(jnp.float32)
        chosen = []
        for m in range(2):
            pick = jnp.where(slot == base + 4.0 * m, 1.0, 0.0).astype(jnp.bfloat16)
            out = jnp.dot(pick, parts[3 * m], preferred_element_type=jnp.float32)
            out = out + jnp.dot(pick, parts[3 * m + 1], preferred_element_type=jnp.float32)
            out = out + jnp.dot(pick, parts[3 * m + 2], preferred_element_type=jnp.float32)
            chosen.append(out.reshape(GROUP, rows, WIDTH))
        a, b = chosen
        for o in range(GROUP):
            d = g * GROUP + o
            send[d, 0:16] = a[o, 0:16]
            send[d, 16:24] = a[o, 16:24] + b[o, 0:8]
            send[d, 24:40] = b[o, 8:24]
        return carry

    with jax.named_scope('build'):
        lax.fori_loop(0, N_DP // GROUP, build, 0)
    with jax.named_scope('barrier'):
        pl.semaphore_wait(barrier, N_DP - 1 + N_PAR - 1)

    core = lax.rem(col, 2)

    def ids(k):
        dz, dx = lax.div(k, NX), lax.rem(k, NX)
        to = lax.rem(z + dz, NZ) * NX + lax.rem(x + dx, NX)
        source_z = lax.rem(z - dz + NZ, NZ)
        source_x = lax.rem(x - dx + NX, NX)
        return to, source_z, source_x

    def pick(table, i):
        return jnp.where(core == 0, table[0][i], table[1][i])

    def block_copy(to, k, landing):
        return pltpu.make_async_remote_copy(
            src_ref=send.at[to], dst_ref=recv.at[landing], send_sem=send_sem, recv_sem=recv_sem.at[k],
            device_id={"dp": to}, device_id_type=MESH)

    def count_copy(to, landing):
        return pltpu.make_async_remote_copy(
            src_ref=cnt_send.at[to], dst_ref=cnt_recv.at[landing], send_sem=cs_sem, recv_sem=cr_sem,
            device_id={"dp": to}, device_id_type=MESH)

    def share_copy(source, source_x, target, from_col):
        return pltpu.make_async_remote_copy(
            src_ref=recv.at[source], dst_ref=share.at[from_col * NX + source_x],
            send_sem=ps_sem, recv_sem=pr_sem.at[from_col * NX + source_x],
            device_id={"parity": target}, device_id_type=MESH)

    with jax.named_scope('issue'):
        for i in range(N_DP - 1):
            k = pick(ISSUE, i)
            to, _, _ = ids(k)
            block_copy(to, k, me).start()
            count_copy(to, me).start()
    recv[me] = send[me]
    cnt_recv[me] = cnt_send[me]

    def place(sz):
        for h in range(NX // 2):
            one, two = sz * NX + 2 * h, sz * NX + 2 * h + 1
            at = pl.ds(pl.multiple_of((sz * (NX // 2) + h) * PAIR, 8), PAIR)
            new_first[at] = jnp.concatenate([recv[one, 0:ROOM], recv[two, 0:ROOM]], axis=0)
            new_second[at] = jnp.concatenate([recv[one, ROOM:PAIR], recv[two, ROOM:PAIR]], axis=0)

    def forward(source, sz, sx):
        @pl.when(sz != col)
        def _():
            share_copy(source, sx, sz, col).start()

    forward(me, z, x)
    for i in range(N_DP - 1):
        k = pick(WAIT, i)
        to, sz, sx = ids(k)
        source = sz * NX + sx
        with jax.named_scope('w'):
            block_copy(to, k, source).wait_recv()
        forward(source, sz, sx)
        for j in range(NZ):
            if PLACED[j] == i:
                place(lax.rem(z - jnp.where(core == 0, PLANES[0][j], PLANES[1][j]) + NZ, NZ))
    with jax.named_scope('counted'):
        sent = pl.ds(0, N_DP - 1)
        pltpu.make_async_remote_copy(
            src_ref=send.at[sent], dst_ref=recv.at[sent], send_sem=send_sem, recv_sem=recv_sem.at[0],
            device_id={"dp": me}, device_id_type=MESH).wait_send()
        pltpu.make_async_remote_copy(
            src_ref=cnt_send.at[sent], dst_ref=cnt_recv.at[sent], send_sem=cs_sem, recv_sem=cr_sem,
            device_id={"dp": me}, device_id_type=MESH).wait()
    total = cnt_recv[0]
    for d in range(1, N_DP):
        total = total + cnt_recv[d]
    loads[...] = total

    away = lax.rem(z - col + NZ, NZ)
    late = jnp.int32(0)
    for dz in range(NZ):
        if DONE[1][dz] < DONE[0][dz]:
            late = jnp.where(away == dz, 1, late)

    def add(member, sx):
        block = share[member * NX + sx]
        for r in range(2):
            c = code_ref[r, member].astype(jnp.float32) * 0.25
            sums[r * NX + sx] = sums[r * NX + sx] + c * block

    for sx in range(NX):
        block = recv[col * NX + sx]
        for r in range(2):
            sums[r * NX + sx] = (code_ref[r, col].astype(jnp.float32) * 0.25) * block

    def shared(j, carry):
        other = 2 * lax.rem(j, 4) + lax.rem(late + lax.div(j, 4), 2)

        @pl.when(other != col)
        def _():
            for sx in range(NX):
                with jax.named_scope('s%d' % sx):
                    share_copy(other * NX + sx, sx, other, other).wait_recv()
                add(other, sx)
        return carry

    lax.fori_loop(0, N_PAR, shared, 0)
    for h in range(NX // 2):
        for r in range(2):
            one, two = sums[r * NX + 2 * h], sums[r * NX + 2 * h + 1]
            at = slice(h * PAIR, (h + 1) * PAIR)
            parity[at, (2 * r) * WIDTH:(2 * r + 1) * WIDTH] = jnp.concatenate([one[0:ROOM], two[0:ROOM]], axis=0)
            parity[at, (2 * r + 1) * WIDTH:(2 * r + 2) * WIDTH] = jnp.concatenate([one[ROOM:PAIR], two[ROOM:PAIR]], axis=0)

    with jax.named_scope('sent'):
        moved = pl.ds(0, (N_PAR - 1) * NX)
        pltpu.make_async_remote_copy(
            src_ref=recv.at[moved], dst_ref=share.at[moved], send_sem=ps_sem, recv_sem=pr_sem.at[0],
            device_id={"parity": col}, device_id_type=MESH).wait_send()


def put_out(nf, ns, par, cnt, nf_out, ns_out, par_out, cnt_out, sem):
    copies = []
    for src, dst, pieces in ((nf, nf_out, PIECES), (ns, ns_out, PIECES), (par, par_out, PIECES // 2)):
        rows = src.shape[0] // pieces
        for n in range(pieces):
            part = pl.ds(n * rows, rows)
            copies.append(pltpu.make_async_copy(src.at[part], dst.at[part], sem.at[len(copies)]))
    for c in copies:
        c.start()
    cnt_out[...] = cnt[0:1, 0:1]
    for c in copies:
        c.wait()


def body(first_moment, second_moment, new_owner, code_index):
    f32, i32 = jnp.float32, jnp.int32
    capacity = N_DP * ROOM
    vmem = pl.BlockSpec(memory_space=pltpu.VMEM)
    anywhere = pl.BlockSpec(memory_space=pl.ANY)
    hbm = pl.BlockSpec(memory_space=pltpu.HBM)
    dma = pltpu.SemaphoreType.DMA
    held = pl.pallas_call(
        exchange,
        out_shape=(jax.ShapeDtypeStruct((capacity, WIDTH), f32), jax.ShapeDtypeStruct((capacity, WIDTH), f32),
                   jax.ShapeDtypeStruct((capacity // N_PAR, 4 * WIDTH), f32), jax.ShapeDtypeStruct((1, 128), i32)),
        in_specs=[hbm, hbm, hbm, hbm],
        out_specs=(vmem, vmem, vmem, vmem),
        scratch_shapes=[
            pltpu.VMEM((1, BLK), i32), pltpu.SMEM((2, N_PAR), i32),
            pltpu.VMEM((BLK, WIDTH), f32), pltpu.VMEM((BLK, WIDTH), f32), pltpu.VMEM((6, BLK, WIDTH), jnp.bfloat16),
            pltpu.VMEM((N_DP, PAIR, WIDTH), f32), pltpu.VMEM((N_DP, PAIR, WIDTH), f32),
            pltpu.VMEM((N_PAR * NX, PAIR, WIDTH), f32), pltpu.VMEM((2 * NX, PAIR, WIDTH), f32),
            pltpu.VMEM((N_DP, 1, 128), i32), pltpu.VMEM((N_DP, 1, 128), i32),
            dma((4,)), dma, dma((N_DP,)), dma, dma, dma, dma((N_DP,)),
        ],
        compiler_params=pltpu.CompilerParams(collective_id=0, has_side_effects=True, vmem_limit_bytes=32 * 2**20),
    )(*(pltpu.with_memory_space_constraint(a, pltpu.HBM)
        for a in (first_moment, second_moment, new_owner.reshape(1, BLK), code_index)))
    return pl.pallas_call(
        put_out,
        out_shape=(jax.ShapeDtypeStruct((capacity, WIDTH), f32), jax.ShapeDtypeStruct((capacity, WIDTH), f32),
                   jax.ShapeDtypeStruct((capacity // N_PAR, 4 * WIDTH), f32), jax.ShapeDtypeStruct((1, 1), i32)),
        in_specs=[vmem, vmem, vmem, vmem],
        out_specs=(anywhere, anywhere, anywhere, vmem),
        scratch_shapes=[dma((2 * PIECES + PIECES // 2,))],
        compiler_params=pltpu.CompilerParams(vmem_limit_bytes=16 * 2**20),
    )(*held)


def solution(mesh):
    rows = P(("dp", "parity"), None)
    return jax.shard_map(body, mesh=mesh, in_specs=(rows, rows, rows, P()),
                         out_specs=(rows, rows, rows, P("dp", "parity")), check_vma=False)
```

time: 92.8 us -> 79.2 us (0.85)
  the two profiles are of different devices: /device:TPU:1 before, /device:TPU:49 now
where the time goes in v2:
time: 79.2 us; the launch traced here: 79.1 us
  Pallas kernels  78.5 us (99%)
    pallas_call x1, Pallas kernels, body(): pl.pallas_call(exchange, out_shape=(jax.ShapeDtypeStruct((capacity, WIDTH...  76.2 us
    pallas_call x1, Pallas kernels, body(): pl.pallas_call(put_out, out_shape=(jax.ShapeDtypeStruct((capacity, WIDTH)...  2.29 us

profile of v2, /device:TPU:49, one launch (start us, length us, event | category | flops | bytes accessed | tf_op | source)
XLA Modules:
  0.0 79.1 jit_solution(10788087758940002412)
XLA Ops:
  0.6 76.2 %shard_map.75 = (f32[640,512]{1,0:T(8,128)S(1)}, f32[640,512]{1,0:T(8,128)S(1)}, f32[80,2048]{1,0:T(8,128)S(1)}, s32[1,128]{1,0:T(1,128)S(1)}) custom-call(f32[512,512]{1,0:T(8,128)} %first_hbm.1, f32[512,512]{1,0:T(8,128)} %second_hbm.1, s32[1,512]{1,0:T(1,128)} %bitcast.1, s32[2,8]{1,0:T(2,128)} %code_hbm.1), custom_call_target="tpu_custom_call" | custom-call | tf_op jit(solution)/shard_map/pallas_call | solution.py:252
  76.8 2.3 %shard_map.76 = (f32[640,512]{1,0:T(8,128)}, f32[640,512]{1,0:T(8,128)}, f32[80,2048]{1,0:T(8,128)}, s32[1,1]{1,0:T(1,128)}) custom-call(f32[640,512]{1,0:T(8,128)S(1)} %get-tuple-element.8.nf, f32[640,512]{1,0:T(8,128)S(1)} %get-tuple-element.9.ns, f32[80,2048]{1,0:T(8,128)S(1)} %get-tuple-element.10.par, s32[1,128]{1,0:T(1,128)S(1)} %get-tuple-element.11.cnt), custom_call_target="tpu_custom_call" | custom-call | tf_op jit(solution)/shard_map/pallas_call | solution.py:269

commit v3 on v2

--- a/solution.py
+++ b/solution.py
@@ -15,30 +15,33 @@
 BLK = 512
 WIDTH = 512
 PAIR = 2 * ROOM
-GROUP = 8
 PIECES = 4
 LANE = 32
 
 
 def by_class(classes):
-    steps = [(0, dx) for dx in range(1, NX)]
-    for c in classes:
+    steps = []
+    for n, c in enumerate(classes):
+        if n == 1:
+            steps += [(0, dx) for dx in range(1, NX)]
         for dx in range(NX):
             steps += [(c, dx)] if 2 * c == NZ else [(c, dx), (NZ - c, dx)]
     return [dz * NX + dx for dz, dx in steps]
 
 
-ISSUE = (by_class((1, 2, 3, 4)), by_class((3, 4, 1, 2)))
+CLASSES = ((1, 2, 4, 3), (1, 4, 3, 2), (1, 3, 4, 2), (1, 4, 2, 3), (1, 3, 4, 2), (1, 4, 2, 3), (1, 3, 2, 4), (1, 3, 4, 2))
+ISSUE = tuple(by_class(c) for c in CLASSES)
 WAIT = ISSUE
 DONE = tuple([max(w.index(k) for k in range(dz * NX, dz * NX + NX) if k) for dz in range(NZ)] for w in WAIT)
 PLANES = tuple(sorted(range(NZ), key=done.__getitem__) for done in DONE)
 PLACED = [max(done[planes[j]] for done, planes in zip(DONE, PLANES)) for j in range(NZ)]
+MEMBERS = tuple(sorted(range(N_PAR), key=lambda p: DONE[p][dz]) for dz in range(NZ))
 
 
 def exchange(first_hbm, second_hbm, owner_hbm, code_hbm,
              new_first, new_second, parity, loads,
              owner_ref, code_ref, x_first, x_second, parts, send, recv, share, sums, cnt_send, cnt_recv,
-             in_sem, send_sem, recv_sem, cs_sem, cr_sem, ps_sem, pr_sem):
+             in_sem, send_sem, recv_sem, cs_sem, cr_sem, ps_sem, pr_sem, ready):
     me = lax.axis_index("dp")
     col = lax.axis_index("parity")
     z = lax.div(me, NX)
@@ -55,11 +58,19 @@
     for c in small_in + loads_in:
         c.start()
 
+    def at(dz, dx):
+        return {"dp": lax.rem(z + dz + NZ, NZ) * NX + lax.rem(x + dx, NX)}
+
+    near = [(dz, dx) for dz in (1, -1, 0) for dx in range(NX) if (dz, dx) != (0, 0)]
     barrier = pltpu.get_barrier_semaphore()
-    for k in range(1, N_DP):
-        pl.semaphore_signal(barrier, inc=1, device_id={"dp": lax.rem(me + k, N_DP)}, device_id_type=MESH)
+    for dz, dx in near:
+        pl.semaphore_signal(barrier, inc=1, device_id=at(dz, dx), device_id_type=MESH)
     for k in range(1, N_PAR):
         pl.semaphore_signal(barrier, inc=1, device_id={"parity": lax.rem(col + k, N_PAR)}, device_id_type=MESH)
+
+    def vouch(sem):
+        for dz in (1, -1):
+            pl.semaphore_signal(sem, inc=1, device_id=at(dz, 0), device_id_type=MESH)
 
     for c in small_in:
         c.wait()
@@ -86,33 +97,28 @@
         parts[3 * m + 2] = (rest - mid.astype(jnp.float32)).astype(jnp.bfloat16)
 
     rows = 24
-    shape = (GROUP, rows, BLK)
+    shape = (NX, rows, BLK)
     slot = (lax.broadcasted_iota(jnp.int32, shape, 0) * LANE + lax.broadcasted_iota(jnp.int32, shape, 1))
-    slot = slot.reshape(GROUP * rows, BLK).astype(jnp.float32)
-
-    def build(g, carry):
-        base = key - (g * (GROUP * LANE)).astype(jnp.float32)
+    slot = slot.reshape(NX * rows, BLK).astype(jnp.float32)
+
+    def build(*planes):
+        planes = [lax.rem(z + dz, NZ) for dz in planes]
         chosen = []
         for m in range(2):
-            pick = jnp.where(slot == base + 4.0 * m, 1.0, 0.0).astype(jnp.bfloat16)
+            pick = jnp.concatenate([
+                jnp.where(slot == key + (4 * m - p * (NX * LANE)).astype(jnp.float32), 1.0, 0.0) for p in planes
+            ], axis=0).astype(jnp.bfloat16)
             out = jnp.dot(pick, parts[3 * m], preferred_element_type=jnp.float32)
             out = out + jnp.dot(pick, parts[3 * m + 1], preferred_element_type=jnp.float32)
             out = out + jnp.dot(pick, parts[3 * m + 2], preferred_element_type=jnp.float32)
-            chosen.append(out.reshape(GROUP, rows, WIDTH))
+            chosen.append(out.reshape(len(planes) * NX, rows, WIDTH))
         a, b = chosen
-        for o in range(GROUP):
-            d = g * GROUP + o
-            send[d, 0:16] = a[o, 0:16]
-            send[d, 16:24] = a[o, 16:24] + b[o, 0:8]
-            send[d, 24:40] = b[o, 8:24]
-        return carry
-
-    with jax.named_scope('build'):
-        lax.fori_loop(0, N_DP // GROUP, build, 0)
-    with jax.named_scope('barrier'):
-        pl.semaphore_wait(barrier, N_DP - 1 + N_PAR - 1)
-
-    core = lax.rem(col, 2)
+        for n, p in enumerate(planes):
+            for o in range(NX):
+                d, o = p * NX + o, n * NX + o
+                send[d, 0:16] = a[o, 0:16]
+                send[d, 16:24] = a[o, 16:24] + b[o, 0:8]
+                send[d, 24:40] = b[o, 8:24]
 
     def ids(k):
         dz, dx = lax.div(k, NX), lax.rem(k, NX)
@@ -121,8 +127,12 @@
         source_x = lax.rem(x - dx + NX, NX)
         return to, source_z, source_x
 
-    def pick(table, i):
-        return jnp.where(core == 0, table[0][i], table[1][i])
+    def pick(table, i, which=col):
+        value = jnp.int32(table[0][i])
+        for p in range(1, len(table)):
+            if table[p][i] != table[0][i]:
+                value = jnp.where(which == p, table[p][i], value)
+        return value
 
     def block_copy(to, k, landing):
         return pltpu.make_async_remote_copy(
@@ -137,15 +147,34 @@
     def share_copy(source, source_x, target, from_col):
         return pltpu.make_async_remote_copy(
             src_ref=recv.at[source], dst_ref=share.at[from_col * NX + source_x],
-            send_sem=ps_sem, recv_sem=pr_sem.at[from_col * NX + source_x],
+            send_sem=ps_sem, recv_sem=pr_sem.at[from_col],
             device_id={"parity": target}, device_id_type=MESH)
 
-    with jax.named_scope('issue'):
-        for i in range(N_DP - 1):
-            k = pick(ISSUE, i)
-            to, _, _ = ids(k)
-            block_copy(to, k, me).start()
-            count_copy(to, me).start()
+    def issue(i):
+        k = pick(ISSUE, i)
+        to, _, _ = ids(k)
+        block_copy(to, k, me).start()
+        count_copy(to, me).start()
+
+    with jax.named_scope('build1'):
+        build(1, NZ - 1)
+    with jax.named_scope('barrier'):
+        pl.semaphore_wait(barrier, len(near) + N_PAR - 1)
+    vouch(ready.at[0])
+    for i in range(2 * NX):
+        issue(i)
+    for c in (2, 3):
+        with jax.named_scope('build%d' % c):
+            build(c, NZ - c)
+        with jax.named_scope('ready%d' % c):
+            pl.semaphore_wait(ready.at[c - 2], 2)
+        vouch(ready.at[c - 1])
+    with jax.named_scope('build4'):
+        build(0, 4)
+    with jax.named_scope('ready4'):
+        pl.semaphore_wait(ready.at[2], 2)
+    for i in range(2 * NX, N_DP - 1):
+        issue(i)
     recv[me] = send[me]
     cnt_recv[me] = cnt_send[me]
 
@@ -171,7 +200,7 @@
         forward(source, sz, sx)
         for j in range(NZ):
             if PLACED[j] == i:
-                place(lax.rem(z - jnp.where(core == 0, PLANES[0][j], PLANES[1][j]) + NZ, NZ))
+                place(lax.rem(z - pick(PLANES, j) + NZ, NZ))
     with jax.named_scope('counted'):
         sent = pl.ds(0, N_DP - 1)
         pltpu.make_async_remote_copy(
@@ -186,10 +215,6 @@
     loads[...] = total
 
     away = lax.rem(z - col + NZ, NZ)
-    late = jnp.int32(0)
-    for dz in range(NZ):
-        if DONE[1][dz] < DONE[0][dz]:
-            late = jnp.where(away == dz, 1, late)
 
     def add(member, sx):
         block = share[member * NX + sx]
@@ -202,18 +227,19 @@
         for r in range(2):
             sums[r * NX + sx] = (code_ref[r, col].astype(jnp.float32) * 0.25) * block
 
-    def shared(j, carry):
-        other = 2 * lax.rem(j, 4) + lax.rem(late + lax.div(j, 4), 2)
+    for j in range(N_PAR):
+        other = pick(MEMBERS, j, away)
 
         @pl.when(other != col)
         def _():
+            four = pl.ds(other * NX, NX)
+            with jax.named_scope('s'):
+                pltpu.make_async_remote_copy(
+                    src_ref=recv.at[four], dst_ref=share.at[four], send_sem=ps_sem, recv_sem=pr_sem.at[other],
+                    device_id={"parity": other}, device_id_type=MESH).wait_recv()
             for sx in range(NX):
-                with jax.named_scope('s%d' % sx):
-                    share_copy(other * NX + sx, sx, other, other).wait_recv()
                 add(other, sx)
-        return carry
-
-    lax.fori_loop(0, N_PAR, shared, 0)
+
     for h in range(NX // 2):
         for r in range(2):
             one, two = sums[r * NX + 2 * h], sums[r * NX + 2 * h + 1]
@@ -228,16 +254,16 @@
             device_id={"parity": col}, device_id_type=MESH).wait_send()
 
 
-def put_out(nf, ns, par, cnt, nf_out, ns_out, par_out, cnt_out, sem):
-    copies = []
+def put_out(nf, ns, par, cnt, nf_out, ns_out, par_out, cnt_out, count, sem):
+    count[...] = cnt[0:1, 0:1]
+    copies = [pltpu.make_async_copy(count, cnt_out, sem.at[0])]
     for src, dst, pieces in ((nf, nf_out, PIECES), (ns, ns_out, PIECES), (par, par_out, PIECES // 2)):
         rows = src.shape[0] // pieces
         for n in range(pieces):
             part = pl.ds(n * rows, rows)
             copies.append(pltpu.make_async_copy(src.at[part], dst.at[part], sem.at[len(copies)]))
-    for c in copies:
+    for c in copies[1:] + copies[:1]:
         c.start()
-    cnt_out[...] = cnt[0:1, 0:1]
     for c in copies:
         c.wait()
 
@@ -261,7 +287,7 @@
             pltpu.VMEM((N_DP, PAIR, WIDTH), f32), pltpu.VMEM((N_DP, PAIR, WIDTH), f32),
             pltpu.VMEM((N_PAR * NX, PAIR, WIDTH), f32), pltpu.VMEM((2 * NX, PAIR, WIDTH), f32),
             pltpu.VMEM((N_DP, 1, 128), i32), pltpu.VMEM((N_DP, 1, 128), i32),
-            dma((4,)), dma, dma((N_DP,)), dma, dma, dma, dma((N_DP,)),
+            dma((4,)), dma, dma((N_DP,)), dma, dma, dma, dma((N_PAR,)), pltpu.SemaphoreType.REGULAR((3,)),
         ],
         compiler_params=pltpu.CompilerParams(collective_id=0, has_side_effects=True, vmem_limit_bytes=32 * 2**20),
     )(*(pltpu.with_memory_space_constraint(a, pltpu.HBM)
@@ -271,8 +297,8 @@
         out_shape=(jax.ShapeDtypeStruct((capacity, WIDTH), f32), jax.ShapeDtypeStruct((capacity, WIDTH), f32),
                    jax.ShapeDtypeStruct((capacity // N_PAR, 4 * WIDTH), f32), jax.ShapeDtypeStruct((1, 1), i32)),
         in_specs=[vmem, vmem, vmem, vmem],
-        out_specs=(anywhere, anywhere, anywhere, vmem),
-        scratch_shapes=[dma((2 * PIECES + PIECES // 2,))],
+        out_specs=(anywhere, anywhere, anywhere, anywhere),
+        scratch_shapes=[pltpu.VMEM((1, 1), i32), dma((1 + 2 * PIECES + PIECES // 2,))],
         compiler_params=pltpu.CompilerParams(vmem_limit_bytes=16 * 2**20),
     )(*held)
 

time: 79.2 us -> 77.4 us (0.977)
  the two profiles are of different devices: /device:TPU:49 before, /device:TPU:16 now
where the time goes in v3:
time: 77.4 us; the launch traced here: 77.3 us
  Pallas kernels  76.6 us (99%)
    pallas_call x1, Pallas kernels, body(): pl.pallas_call(exchange, out_shape=(jax.ShapeDtypeStruct((capacity, WIDTH...  74.8 us
    pallas_call x1, Pallas kernels, body(): pl.pallas_call(put_out, out_shape=(jax.ShapeDtypeStruct((capacity, WIDTH)...  1.79 us

profile of v3, /device:TPU:16, one launch (start us, length us, event | category | flops | bytes accessed | tf_op | source)
XLA Modules:
  0.0 77.3 jit_solution(10615331595620415115)
XLA Ops:
  0.6 74.8 %shard_map.75 = (f32[640,512]{1,0:T(8,128)S(1)}, f32[640,512]{1,0:T(8,128)S(1)}, f32[80,2048]{1,0:T(8,128)S(1)}, s32[1,128]{1,0:T(1,128)S(1)}) custom-call(f32[512,512]{1,0:T(8,128)} %first_hbm.1, f32[512,512]{1,0:T(8,128)} %second_hbm.1, s32[1,512]{1,0:T(1,128)} %bitcast.1, s32[2,8]{1,0:T(2,128)} %code_hbm.1), custom_call_target="tpu_custom_call" | custom-call | tf_op jit(solution)/shard_map/pallas_call | solution.py:278
  75.5 1.8 %shard_map.76 = (f32[640,512]{1,0:T(8,128)}, f32[640,512]{1,0:T(8,128)}, f32[80,2048]{1,0:T(8,128)}, s32[1,1]{1,0:T(1,128)}) custom-call(f32[640,512]{1,0:T(8,128)S(1)} %get-tuple-element.8.nf, f32[640,512]{1,0:T(8,128)S(1)} %get-tuple-element.9.ns, f32[80,2048]{1,0:T(8,128)S(1)} %get-tuple-element.10.par, s32[1,128]{1,0:T(1,128)S(1)} %get-tuple-element.11.cnt), custom_call_target="tpu_custom_call" | custom-call | tf_op jit(solution)/shard_map/pallas_call | solution.py:295

commit v4 on v3

--- a/solution.py
+++ b/solution.py
@@ -19,18 +19,16 @@
 LANE = 32
 
 
-def by_class(classes):
-    steps = []
-    for n, c in enumerate(classes):
-        if n == 1:
-            steps += [(0, dx) for dx in range(1, NX)]
-        for dx in range(NX):
-            steps += [(c, dx)] if 2 * c == NZ else [(c, dx), (NZ - c, dx)]
-    return [dz * NX + dx for dz, dx in steps]
-
-
-CLASSES = ((1, 2, 4, 3), (1, 4, 3, 2), (1, 3, 4, 2), (1, 4, 2, 3), (1, 3, 4, 2), (1, 4, 2, 3), (1, 3, 2, 4), (1, 3, 4, 2))
-ISSUE = tuple(by_class(c) for c in CLASSES)
+ISSUE = (
+    (4, 28, 5, 29, 6, 30, 7, 31, 1, 2, 3, 9, 25, 17, 13, 21, 11, 27, 19, 15, 23, 10, 26, 18, 14, 22, 8, 24, 16, 12, 20),
+    (4, 28, 5, 29, 6, 30, 7, 31, 1, 2, 3, 12, 20, 16, 8, 24, 13, 21, 17, 9, 25, 14, 22, 18, 10, 26, 15, 23, 19, 11, 27),
+    (4, 28, 5, 29, 6, 30, 7, 31, 1, 2, 3, 17, 13, 21, 9, 25, 19, 15, 23, 11, 27, 18, 14, 22, 10, 26, 16, 12, 20, 8, 24),
+    (4, 28, 5, 29, 6, 30, 7, 31, 1, 2, 3, 8, 24, 12, 20, 16, 9, 25, 13, 21, 17, 10, 26, 14, 22, 18, 11, 27, 15, 23, 19),
+    (4, 28, 5, 29, 6, 30, 7, 31, 1, 2, 3, 13, 21, 9, 25, 17, 15, 23, 11, 27, 19, 14, 22, 10, 26, 18, 12, 20, 8, 24, 16),
+    (4, 28, 5, 29, 6, 30, 7, 31, 1, 2, 3, 16, 8, 24, 12, 20, 17, 9, 25, 15, 23, 13, 21, 18, 10, 26, 19, 14, 22, 11, 27),
+    (4, 28, 5, 29, 6, 30, 7, 31, 1, 2, 3, 9, 25, 17, 13, 21, 11, 27, 19, 15, 23, 10, 26, 18, 14, 22, 8, 24, 16, 12, 20),
+    (4, 28, 5, 29, 6, 30, 7, 31, 1, 2, 3, 12, 20, 16, 8, 24, 13, 21, 17, 9, 25, 14, 22, 18, 10, 26, 15, 23, 19, 11, 27),
+)
 WAIT = ISSUE
 DONE = tuple([max(w.index(k) for k in range(dz * NX, dz * NX + NX) if k) for dz in range(NZ)] for w in WAIT)
 PLANES = tuple(sorted(range(NZ), key=done.__getitem__) for done in DONE)
@@ -39,8 +37,8 @@
 
 
 def exchange(first_hbm, second_hbm, owner_hbm, code_hbm,
-             new_first, new_second, parity, loads,
-             owner_ref, code_ref, x_first, x_second, parts, send, recv, share, sums, cnt_send, cnt_recv,
+             new_first, new_second, sums, loads,
+             owner_ref, code_ref, x_first, x_second, earlier, parts, send, recv, share, cnt_send, cnt_recv,
              in_sem, send_sem, recv_sem, cs_sem, cr_sem, ps_sem, pr_sem, ready):
     me = lax.axis_index("dp")
     col = lax.axis_index("parity")
@@ -72,20 +70,46 @@
         for dz in (1, -1):
             pl.semaphore_signal(sem, inc=1, device_id=at(dz, 0), device_id_type=MESH)
 
+    earlier[...] = (lax.broadcasted_iota(jnp.int32, (BLK, BLK), 0)
+                    < lax.broadcasted_iota(jnp.int32, (BLK, BLK), 1)).astype(jnp.float32).astype(jnp.bfloat16)
     for c in small_in:
         c.wait()
     owner = owner_ref[...]
     onehot = (lax.broadcasted_iota(jnp.int32, (N_DP, BLK), 0) == owner).astype(jnp.float32)
-    earlier = lax.broadcasted_iota(jnp.int32, (BLK, BLK), 0) < lax.broadcasted_iota(jnp.int32, (BLK, BLK), 1)
-    before = jnp.dot(onehot.astype(jnp.bfloat16), earlier.astype(jnp.float32).astype(jnp.bfloat16),
-                     preferred_element_type=jnp.float32)
+    before = jnp.dot(onehot.astype(jnp.bfloat16), earlier[...], preferred_element_type=jnp.float32)
     rank = jnp.sum(before * onehot, axis=0, keepdims=True)
     key = owner.astype(jnp.float32) * LANE + rank
-    counts = jnp.sum(onehot, axis=1, keepdims=True).astype(jnp.int32)
-    counts = jnp.broadcast_to(counts, (N_DP, 128))
-    for d in range(N_DP):
-        cnt_send[d] = counts[d:d + 1]
-
+
+    rows = 24
+    shape = (NX, rows, BLK)
+    slot = (lax.broadcasted_iota(jnp.int32, shape, 0) * LANE + lax.broadcasted_iota(jnp.int32, shape, 1))
+    slot = slot.reshape(NX * rows, BLK).astype(jnp.float32)
+
+    def choose(m, planes):
+        chosen = jnp.concatenate([
+            jnp.where(slot == key + (4 * m - p * (NX * LANE)).astype(jnp.float32), 1.0, 0.0) for p in planes
+        ], axis=0).astype(jnp.bfloat16)
+        out = jnp.dot(chosen, parts[3 * m], preferred_element_type=jnp.float32)
+        out = out + jnp.dot(chosen, parts[3 * m + 1], preferred_element_type=jnp.float32)
+        out = out + jnp.dot(chosen, parts[3 * m + 2], preferred_element_type=jnp.float32)
+        return out.reshape(len(planes) * NX, rows, WIDTH)
+
+    def fill(planes, a, b):
+        for n, p in enumerate(planes):
+            for o in range(NX):
+                d, o = p * NX + o, n * NX + o
+                send[d, 0:16] = a[o, 0:16]
+                send[d, 16:24] = a[o, 16:24] + b[o, 0:8]
+                send[d, 24:40] = b[o, 8:24]
+
+    def planes_at(*distances):
+        return [lax.rem(z + dz, NZ) for dz in distances]
+
+    def build(*distances):
+        planes = planes_at(*distances)
+        fill(planes, choose(0, planes), choose(1, planes))
+
+    beside, built = planes_at(1, NZ - 1), []
     for m, (c, src) in enumerate(zip(loads_in, (x_first, x_second))):
         c.wait()
         whole = src[...]
@@ -95,30 +119,8 @@
         parts[3 * m] = high
         parts[3 * m + 1] = mid
         parts[3 * m + 2] = (rest - mid.astype(jnp.float32)).astype(jnp.bfloat16)
-
-    rows = 24
-    shape = (NX, rows, BLK)
-    slot = (lax.broadcasted_iota(jnp.int32, shape, 0) * LANE + lax.broadcasted_iota(jnp.int32, shape, 1))
-    slot = slot.reshape(NX * rows, BLK).astype(jnp.float32)
-
-    def build(*planes):
-        planes = [lax.rem(z + dz, NZ) for dz in planes]
-        chosen = []
-        for m in range(2):
-            pick = jnp.concatenate([
-                jnp.where(slot == key + (4 * m - p * (NX * LANE)).astype(jnp.float32), 1.0, 0.0) for p in planes
-            ], axis=0).astype(jnp.bfloat16)
-            out = jnp.dot(pick, parts[3 * m], preferred_element_type=jnp.float32)
-            out = out + jnp.dot(pick, parts[3 * m + 1], preferred_element_type=jnp.float32)
-            out = out + jnp.dot(pick, parts[3 * m + 2], preferred_element_type=jnp.float32)
-            chosen.append(out.reshape(len(planes) * NX, rows, WIDTH))
-        a, b = chosen
-        for n, p in enumerate(planes):
-            for o in range(NX):
-                d, o = p * NX + o, n * NX + o
-                send[d, 0:16] = a[o, 0:16]
-                send[d, 16:24] = a[o, 16:24] + b[o, 0:8]
-                send[d, 24:40] = b[o, 8:24]
+        built.append(choose(m, beside))
+    fill(beside, *built)
 
     def ids(k):
         dz, dx = lax.div(k, NX), lax.rem(k, NX)
@@ -156,8 +158,10 @@
         block_copy(to, k, me).start()
         count_copy(to, me).start()
 
-    with jax.named_scope('build1'):
-        build(1, NZ - 1)
+    counts = jnp.sum(onehot, axis=1, keepdims=True).astype(jnp.int32)
+    counts = jnp.broadcast_to(counts, (N_DP, 128))
+    for d in range(N_DP):
+        cnt_send[d] = counts[d:d + 1]
     with jax.named_scope('barrier'):
         pl.semaphore_wait(barrier, len(near) + N_PAR - 1)
     vouch(ready.at[0])
@@ -240,30 +244,33 @@
             for sx in range(NX):
                 add(other, sx)
 
+    with jax.named_scope('sent'):
+        moved = pl.ds(0, (N_PAR - 1) * NX)
+        pltpu.make_async_remote_copy(
+            src_ref=recv.at[moved], dst_ref=share.at[moved], send_sem=ps_sem, recv_sem=pr_sem.at[0],
+            device_id={"parity": col}, device_id_type=MESH).wait_send()
+
+
+def put_out(nf, ns, sums, cnt, nf_out, ns_out, par_out, cnt_out, count, parity, sem):
+    copies = []
+    for src, dst in ((nf, nf_out), (ns, ns_out)):
+        rows = src.shape[0] // PIECES
+        for n in range(PIECES):
+            part = pl.ds(n * rows, rows)
+            copies.append(pltpu.make_async_copy(src.at[part], dst.at[part], sem.at[len(copies)]))
+            copies[-1].start()
+    count[...] = cnt[0:1, 0:1]
+    copies.append(pltpu.make_async_copy(count, cnt_out, sem.at[len(copies)]))
+    copies[-1].start()
     for h in range(NX // 2):
         for r in range(2):
             one, two = sums[r * NX + 2 * h], sums[r * NX + 2 * h + 1]
             at = slice(h * PAIR, (h + 1) * PAIR)
             parity[at, (2 * r) * WIDTH:(2 * r + 1) * WIDTH] = jnp.concatenate([one[0:ROOM], two[0:ROOM]], axis=0)
             parity[at, (2 * r + 1) * WIDTH:(2 * r + 2) * WIDTH] = jnp.concatenate([one[ROOM:PAIR], two[ROOM:PAIR]], axis=0)
-
-    with jax.named_scope('sent'):
-        moved = pl.ds(0, (N_PAR - 1) * NX)
-        pltpu.make_async_remote_copy(
-            src_ref=recv.at[moved], dst_ref=share.at[moved], send_sem=ps_sem, recv_sem=pr_sem.at[0],
-            device_id={"parity": col}, device_id_type=MESH).wait_send()
-
-
-def put_out(nf, ns, par, cnt, nf_out, ns_out, par_out, cnt_out, count, sem):
-    count[...] = cnt[0:1, 0:1]
-    copies = [pltpu.make_async_copy(count, cnt_out, sem.at[0])]
-    for src, dst, pieces in ((nf, nf_out, PIECES), (ns, ns_out, PIECES), (par, par_out, PIECES // 2)):
-        rows = src.shape[0] // pieces
-        for n in range(pieces):
-            part = pl.ds(n * rows, rows)
-            copies.append(pltpu.make_async_copy(src.at[part], dst.at[part], sem.at[len(copies)]))
-    for c in copies[1:] + copies[:1]:
-        c.start()
+        part = pl.ds(h * PAIR, PAIR)
+        copies.append(pltpu.make_async_copy(parity.at[part], par_out.at[part], sem.at[len(copies)]))
+        copies[-1].start()
     for c in copies:
         c.wait()
 
@@ -278,14 +285,15 @@
     held = pl.pallas_call(
         exchange,
         out_shape=(jax.ShapeDtypeStruct((capacity, WIDTH), f32), jax.ShapeDtypeStruct((capacity, WIDTH), f32),
-                   jax.ShapeDtypeStruct((capacity // N_PAR, 4 * WIDTH), f32), jax.ShapeDtypeStruct((1, 128), i32)),
+                   jax.ShapeDtypeStruct((2 * NX, PAIR, WIDTH), f32), jax.ShapeDtypeStruct((1, 128), i32)),
         in_specs=[hbm, hbm, hbm, hbm],
         out_specs=(vmem, vmem, vmem, vmem),
         scratch_shapes=[
             pltpu.VMEM((1, BLK), i32), pltpu.SMEM((2, N_PAR), i32),
-            pltpu.VMEM((BLK, WIDTH), f32), pltpu.VMEM((BLK, WIDTH), f32), pltpu.VMEM((6, BLK, WIDTH), jnp.bfloat16),
+            pltpu.VMEM((BLK, WIDTH), f32), pltpu.VMEM((BLK, WIDTH), f32), pltpu.VMEM((BLK, BLK), jnp.bfloat16),
+            pltpu.VMEM((6, BLK, WIDTH), jnp.bfloat16),
             pltpu.VMEM((N_DP, PAIR, WIDTH), f32), pltpu.VMEM((N_DP, PAIR, WIDTH), f32),
-            pltpu.VMEM((N_PAR * NX, PAIR, WIDTH), f32), pltpu.VMEM((2 * NX, PAIR, WIDTH), f32),
+            pltpu.VMEM((N_PAR * NX, PAIR, WIDTH), f32),
             pltpu.VMEM((N_DP, 1, 128), i32), pltpu.VMEM((N_DP, 1, 128), i32),
             dma((4,)), dma, dma((N_DP,)), dma, dma, dma, dma((N_PAR,)), pltpu.SemaphoreType.REGULAR((3,)),
         ],
@@ -298,7 +306,8 @@
                    jax.ShapeDtypeStruct((capacity // N_PAR, 4 * WIDTH), f32), jax.ShapeDtypeStruct((1, 1), i32)),
         in_specs=[vmem, vmem, vmem, vmem],
         out_specs=(anywhere, anywhere, anywhere, anywhere),
-        scratch_shapes=[pltpu.VMEM((1, 1), i32), dma((1 + 2 * PIECES + PIECES // 2,))],
+        scratch_shapes=[pltpu.VMEM((1, 1), i32), pltpu.VMEM((capacity // N_PAR, 4 * WIDTH), f32),
+                        dma((2 * PIECES + 1 + NX // 2,))],
         compiler_params=pltpu.CompilerParams(vmem_limit_bytes=16 * 2**20),
     )(*held)
 

time: 77.4 us -> 76.2 us (0.984)
  the two profiles are of different devices: /device:TPU:16 before, /device:TPU:13 now
where the time goes in v4:
time: 76.2 us; the launch traced here: 76.1 us
  Pallas kernels  75.4 us (99%)
    pallas_call x1, Pallas kernels, body(): pl.pallas_call(exchange, out_shape=(jax.ShapeDtypeStruct((capacity, WIDTH...  73.6 us
    pallas_call x1, Pallas kernels, body(): pl.pallas_call(put_out, out_shape=(jax.ShapeDtypeStruct((capacity, WIDTH)...  1.8 us

profile of v4, /device:TPU:13, one launch (start us, length us, event | category | flops | bytes accessed | tf_op | source)
XLA Modules:
  0.0 76.1 jit_solution(9056200664849653620)
XLA Ops:
  0.6 73.6 %shard_map.75 = (f32[640,512]{1,0:T(8,128)S(1)}, f32[640,512]{1,0:T(8,128)S(1)}, f32[8,40,512]{2,1,0:T(8,128)S(1)}, s32[1,128]{1,0:T(1,128)S(1)}) custom-call(f32[512,512]{1,0:T(8,128)} %first_hbm.1, f32[512,512]{1,0:T(8,128)} %second_hbm.1, s32[1,512]{1,0:T(1,128)} %bitcast.1, s32[2,8]{1,0:T(2,128)} %code_hbm.1), custom_call_target="tpu_custom_call" | custom-call | tf_op jit(solution)/shard_map/pallas_call | solution.py:285
  74.3 1.8 %shard_map.76 = (f32[640,512]{1,0:T(8,128)}, f32[640,512]{1,0:T(8,128)}, f32[80,2048]{1,0:T(8,128)}, s32[1,1]{1,0:T(1,128)}) custom-call(f32[640,512]{1,0:T(8,128)S(1)} %get-tuple-element.8.nf, f32[640,512]{1,0:T(8,128)S(1)} %get-tuple-element.9.ns, f32[8,40,512]{2,1,0:T(8,128)S(1)} %get-tuple-element.10.sums, s32[1,128]{1,0:T(1,128)S(1)} %get-tuple-element.11.cnt), custom_call_target="tpu_custom_call" | custom-call | tf_op jit(solution)/shard_map/pallas_call | solution.py:303

commit v5 on v4

--- a/solution.py
+++ b/solution.py
@@ -23,7 +23,7 @@
     (4, 28, 5, 29, 6, 30, 7, 31, 1, 2, 3, 9, 25, 17, 13, 21, 11, 27, 19, 15, 23, 10, 26, 18, 14, 22, 8, 24, 16, 12, 20),
     (4, 28, 5, 29, 6, 30, 7, 31, 1, 2, 3, 12, 20, 16, 8, 24, 13, 21, 17, 9, 25, 14, 22, 18, 10, 26, 15, 23, 19, 11, 27),
     (4, 28, 5, 29, 6, 30, 7, 31, 1, 2, 3, 17, 13, 21, 9, 25, 19, 15, 23, 11, 27, 18, 14, 22, 10, 26, 16, 12, 20, 8, 24),
-    (4, 28, 5, 29, 6, 30, 7, 31, 1, 2, 3, 8, 24, 12, 20, 16, 9, 25, 13, 21, 17, 10, 26, 14, 22, 18, 11, 27, 15, 23, 19),
+    (4, 28, 5, 29, 6, 30, 7, 31, 1, 2, 3, 16, 17, 18, 19, 8, 24, 9, 25, 10, 26, 11, 27, 12, 20, 13, 21, 14, 22, 15, 23),
     (4, 28, 5, 29, 6, 30, 7, 31, 1, 2, 3, 13, 21, 9, 25, 17, 15, 23, 11, 27, 19, 14, 22, 10, 26, 18, 12, 20, 8, 24, 16),
     (4, 28, 5, 29, 6, 30, 7, 31, 1, 2, 3, 16, 8, 24, 12, 20, 17, 9, 25, 15, 23, 13, 21, 18, 10, 26, 19, 14, 22, 11, 27),
     (4, 28, 5, 29, 6, 30, 7, 31, 1, 2, 3, 9, 25, 17, 13, 21, 11, 27, 19, 15, 23, 10, 26, 18, 14, 22, 8, 24, 16, 12, 20),

time: 76.2 us -> 76.1 us (level)
  no operation moved by 1% of the time
where the time goes in v5:
time: 76.1 us; the launch traced here: 76 us
  Pallas kernels  75.4 us (99%)
    pallas_call x1, Pallas kernels, body(): pl.pallas_call(exchange, out_shape=(jax.ShapeDtypeStruct((capacity, WIDTH...  73.6 us
    pallas_call x1, Pallas kernels, body(): pl.pallas_call(put_out, out_shape=(jax.ShapeDtypeStruct((capacity, WIDTH)...  1.8 us

profile of v5, /device:TPU:13, one launch (start us, length us, event | category | flops | bytes accessed | tf_op | source)
XLA Modules:
  0.0 76.0 jit_solution(14602370444819704951)
XLA Ops:
  0.6 73.6 %shard_map.75 = (f32[640,512]{1,0:T(8,128)S(1)}, f32[640,512]{1,0:T(8,128)S(1)}, f32[8,40,512]{2,1,0:T(8,128)S(1)}, s32[1,128]{1,0:T(1,128)S(1)}) custom-call(f32[512,512]{1,0:T(8,128)} %first_hbm.1, f32[512,512]{1,0:T(8,128)} %second_hbm.1, s32[1,512]{1,0:T(1,128)} %bitcast.1, s32[2,8]{1,0:T(2,128)} %code_hbm.1), custom_call_target="tpu_custom_call" | custom-call | tf_op jit(solution)/shard_map/pallas_call | solution.py:285
  74.2 1.8 %shard_map.76 = (f32[640,512]{1,0:T(8,128)}, f32[640,512]{1,0:T(8,128)}, f32[80,2048]{1,0:T(8,128)}, s32[1,1]{1,0:T(1,128)}) custom-call(f32[640,512]{1,0:T(8,128)S(1)} %get-tuple-element.8.nf, f32[640,512]{1,0:T(8,128)S(1)} %get-tuple-element.9.ns, f32[8,40,512]{2,1,0:T(8,128)S(1)} %get-tuple-element.10.sums, s32[1,128]{1,0:T(1,128)S(1)} %get-tuple-element.11.cnt), custom_call_target="tpu_custom_call" | custom-call | tf_op jit(solution)/shard_map/pallas_call | solution.py:303

commit v6 on v5

--- a/solution.py
+++ b/solution.py
@@ -15,7 +15,7 @@
 BLK = 512
 WIDTH = 512
 PAIR = 2 * ROOM
-PIECES = 4
+PIECES = 1
 LANE = 32
 
 
@@ -156,17 +156,16 @@
         k = pick(ISSUE, i)
         to, _, _ = ids(k)
         block_copy(to, k, me).start()
-        count_copy(to, me).start()
-
-    counts = jnp.sum(onehot, axis=1, keepdims=True).astype(jnp.int32)
-    counts = jnp.broadcast_to(counts, (N_DP, 128))
-    for d in range(N_DP):
-        cnt_send[d] = counts[d:d + 1]
+
     with jax.named_scope('barrier'):
         pl.semaphore_wait(barrier, len(near) + N_PAR - 1)
     vouch(ready.at[0])
     for i in range(2 * NX):
         issue(i)
+    counts = jnp.sum(onehot, axis=1, keepdims=True).astype(jnp.int32)
+    counts = jnp.broadcast_to(counts, (N_DP, 128))
+    for d in range(N_DP):
+        cnt_send[d] = counts[d:d + 1]
     for c in (2, 3):
         with jax.named_scope('build%d' % c):
             build(c, NZ - c)
@@ -179,6 +178,9 @@
         pl.semaphore_wait(ready.at[2], 2)
     for i in range(2 * NX, N_DP - 1):
         issue(i)
+    for i in range(N_DP - 1):
+        to, _, _ = ids(pick(ISSUE, i))
+        count_copy(to, me).start()
     recv[me] = send[me]
     cnt_recv[me] = cnt_send[me]
 

time: 76.1 us -> 76 us (level)
  no operation moved by 1% of the time
where the time goes in v6:
time: 76 us; the launch traced here: 75.9 us
  Pallas kernels  75.2 us (99%)
    pallas_call x1, Pallas kernels, body(): pl.pallas_call(exchange, out_shape=(jax.ShapeDtypeStruct((capacity, WIDTH...  73.5 us
    pallas_call x1, Pallas kernels, body(): pl.pallas_call(put_out, out_shape=(jax.ShapeDtypeStruct((capacity, WIDTH)...  1.75 us

profile of v6, /device:TPU:13, one launch (start us, length us, event | category | flops | bytes accessed | tf_op | source)
XLA Modules:
  0.0 75.9 jit_solution(2280076568657906440)
XLA Ops:
  0.6 73.5 %shard_map.75 = (f32[640,512]{1,0:T(8,128)S(1)}, f32[640,512]{1,0:T(8,128)S(1)}, f32[8,40,512]{2,1,0:T(8,128)S(1)}, s32[1,128]{1,0:T(1,128)S(1)}) custom-call(f32[512,512]{1,0:T(8,128)} %first_hbm.1, f32[512,512]{1,0:T(8,128)} %second_hbm.1, s32[1,512]{1,0:T(1,128)} %bitcast.1, s32[2,8]{1,0:T(2,128)} %code_hbm.1), custom_call_target="tpu_custom_call" | custom-call | tf_op jit(solution)/shard_map/pallas_call | solution.py:287
  74.1 1.7 %shard_map.76 = (f32[640,512]{1,0:T(8,128)}, f32[640,512]{1,0:T(8,128)}, f32[80,2048]{1,0:T(8,128)}, s32[1,1]{1,0:T(1,128)}) custom-call(f32[640,512]{1,0:T(8,128)S(1)} %get-tuple-element.8.nf, f32[640,512]{1,0:T(8,128)S(1)} %get-tuple-element.9.ns, f32[8,40,512]{2,1,0:T(8,128)S(1)} %get-tuple-element.10.sums, s32[1,128]{1,0:T(1,128)S(1)} %get-tuple-element.11.cnt), custom_call_target="tpu_custom_call" | custom-call | tf_op jit(solution)/shard_map/pallas_call | solution.py:305

commit v7 on v6

--- a/solution.py
+++ b/solution.py
@@ -167,11 +167,11 @@
     for d in range(N_DP):
         cnt_send[d] = counts[d:d + 1]
     for c in (2, 3):
-        with jax.named_scope('build%d' % c):
-            build(c, NZ - c)
         with jax.named_scope('ready%d' % c):
             pl.semaphore_wait(ready.at[c - 2], 2)
         vouch(ready.at[c - 1])
+        with jax.named_scope('build%d' % c):
+            build(c, NZ - c)
     with jax.named_scope('build4'):
         build(0, 4)
     with jax.named_scope('ready4'):

time: 76 us -> 75.7 us (level)
  no operation moved by 1% of the time
where the time goes in v7:
time: 75.7 us; the launch traced here: 75.5 us
  Pallas kernels  74.9 us (99%)
    pallas_call x1, Pallas kernels, body(): pl.pallas_call(exchange, out_shape=(jax.ShapeDtypeStruct((capacity, WIDTH...  73.2 us
    pallas_call x1, Pallas kernels, body(): pl.pallas_call(put_out, out_shape=(jax.ShapeDtypeStruct((capacity, WIDTH)...  1.75 us

profile of v7, /device:TPU:13, one launch (start us, length us, event | category | flops | bytes accessed | tf_op | source)
XLA Modules:
  0.0 75.5 jit_solution(14353698852798009417)
XLA Ops:
  0.6 73.2 %shard_map.75 = (f32[640,512]{1,0:T(8,128)S(1)}, f32[640,512]{1,0:T(8,128)S(1)}, f32[8,40,512]{2,1,0:T(8,128)S(1)}, s32[1,128]{1,0:T(1,128)S(1)}) custom-call(f32[512,512]{1,0:T(8,128)} %first_hbm.1, f32[512,512]{1,0:T(8,128)} %second_hbm.1, s32[1,512]{1,0:T(1,128)} %bitcast.1, s32[2,8]{1,0:T(2,128)} %code_hbm.1), custom_call_target="tpu_custom_call" | custom-call | tf_op jit(solution)/shard_map/pallas_call | solution.py:287
  73.8 1.7 %shard_map.76 = (f32[640,512]{1,0:T(8,128)}, f32[640,512]{1,0:T(8,128)}, f32[80,2048]{1,0:T(8,128)}, s32[1,1]{1,0:T(1,128)}) custom-call(f32[640,512]{1,0:T(8,128)S(1)} %get-tuple-element.8.nf, f32[640,512]{1,0:T(8,128)S(1)} %get-tuple-element.9.ns, f32[8,40,512]{2,1,0:T(8,128)S(1)} %get-tuple-element.10.sums, s32[1,128]{1,0:T(1,128)S(1)} %get-tuple-element.11.cnt), custom_call_target="tpu_custom_call" | custom-call | tf_op jit(solution)/shard_map/pallas_call | solution.py:305
